TPU v7x, 32 devices: a whole 2x2x4 slice. The times are simulated.
32 devices in a mesh: img: 2 (over x), rows: 16 (over z, y, core).
Axes of the slice: x: 2, y: 2, z: 4, core: 2. Of those that a mesh axis runs over, the one named last changes fastest.
Arguments:
- image: bfloat16 [128, 256, 512], P(('img', 'rows')), parts along dimension 0, may hold values from -32 to 32
- gain_in: float32 [512], replicated, may hold values from 0.1 to 1.9
- shift_in: float32 [512], replicated, may hold values from -3 to 3
- conv_in: bfloat16 [3, 3, 512, 512], replicated, may hold values from -0.09375 to 0.09375
- gain_mid: float32 [512], replicated, may hold values from 0.1 to 1.9
- shift_mid: float32 [512], replicated, may hold values from -3 to 3
- conv_out: bfloat16 [3, 3, 512, 512], replicated, may hold values from -0.09375 to 0.09375
- bias_out: float32 [512], replicated, may hold values from -2 to 2
Outputs:
- result: bfloat16 [128, 256, 512], P(('img', 'rows')), parts along dimension 0
There are 2 independent parts, one for each index of `img`. A program takes and returns all parts, laid end to end along the dimension named above; an argument that names none is the same for every part. Nothing has to cross between parts.
All inputs are finite; a program needn't handle non-finite values.
Results may differ from a plain program's by a relative error of at most 0.0045.
Values may be sent and summed in bfloat16 or wider, within the bound.
A program may use at most 64 MiB of HBM per device.

v0:
```python
import functools

import jax
import jax.numpy as jnp
from jax import lax
from jax.experimental import pallas as pl
from jax.experimental.pallas import tpu as pltpu
from jax.sharding import PartitionSpec as P

GROUPS = 32
LANES = 128
CHUNK = 32
TILE = 256
MESH = pl.DeviceIdType.MESH


def packed(sums, squares):
    chans = sums.shape[1]
    pieces = [part[:, k : k + LANES] for part in (sums, squares) for k in range(0, chans, LANES)]
    return jnp.concatenate(pieces, axis=0)


def flat(tile):
    return jnp.concatenate([tile[k : k + 1] for k in range(tile.shape[0])], axis=1)


def group_total(tile, size):
    lane = lax.broadcasted_iota(jnp.int32, tile.shape, 1)
    step = 1
    while step < size:
        up = pltpu.roll(tile, step, 1)
        down = pltpu.roll(tile, LANES - step, 1)
        tile = tile + jnp.where((lane & step) != 0, up, down)
        step *= 2
    return tile


def kernel(n, image, gain_in, shift_in, conv_in, gain_mid, shift_mid, conv_out, bias_out, out,
           img, act, mid, result, w_in, w_out, w_mix, v_mix, acc, gath_in, gath_mid,
           local_sem, out_sem, halo_send, halo_recv, stat_send, stat_recv):
    me = lax.axis_index("rows")
    height, width, chans = image.shape
    count = float(height * width * (chans // GROUPS) * n)
    parts = chans // LANES

    load = pltpu.make_async_copy(image, img.at[pl.ds(1, height)], local_sem.at[0])
    load.start()
    load_w_in = pltpu.make_async_copy(conv_in, w_in, local_sem.at[1])
    load_w_in.start()
    load_w_out = pltpu.make_async_copy(conv_out, w_out, local_sem.at[2])
    load_w_out.start()

    barrier = pltpu.get_barrier_semaphore()
    for d in range(1, n):
        pl.semaphore_signal(
            barrier, inc=1, device_id={"rows": lax.rem(me + d, n)}, device_id_type=MESH
        )

    def add_stats(value, lanes):
        rows = value.shape[0]
        folded = value.reshape(rows // 8, 8, value.shape[1])
        acc[0, :, lanes] += jnp.sum(folded, axis=0)
        acc[1, :, lanes] += jnp.sum(folded * folded, axis=0)

    def stat_copy(gath, which, d):
        return pltpu.make_async_remote_copy(
            src_ref=gath.at[0],
            dst_ref=gath.at[d],
            send_sem=stat_send.at[which, d],
            recv_sem=stat_recv.at[which, d],
            device_id={"rows": lax.rem(me + d, n)},
            device_id_type=MESH,
        )

    def send_stats(gath, which):
        sums = jnp.sum(acc[0], axis=0, keepdims=True)
        squares = jnp.sum(acc[1], axis=0, keepdims=True)
        gath[0] = packed(sums, squares)
        for d in range(1, n):
            stat_copy(gath, which, d).start()

    def receive_stats(gath, which, gain):
        for d in range(1, n):
            stat_copy(gath, which, d).wait()
        total = group_total(jnp.sum(gath[...], axis=0), chans // GROUPS) / count
        mean, square = total[:parts], total[parts:]
        variance = jnp.maximum(square - mean * mean, 0.0)
        return flat(mean), flat(lax.rsqrt(variance + 1e-06)) * (0.5 * gain[...])

    def halo_copies(buf, which):
        up = pltpu.make_async_remote_copy(
            src_ref=buf.at[1],
            dst_ref=buf.at[height + 1],
            send_sem=halo_send.at[which, 0],
            recv_sem=halo_recv.at[which, 0],
            device_id={"rows": jnp.maximum(me - 1, 0)},
            device_id_type=MESH,
        )
        down = pltpu.make_async_remote_copy(
            src_ref=buf.at[height],
            dst_ref=buf.at[0],
            send_sem=halo_send.at[which, 1],
            recv_sem=halo_recv.at[which, 1],
            device_id={"rows": jnp.minimum(me + 1, n - 1)},
            device_id_type=MESH,
        )
        return up, down

    def send_halo(buf, which):
        up, down = halo_copies(buf, which)

        @pl.when(me > 0)
        def _():
            up.start()

        @pl.when(me < n - 1)
        def _():
            down.start()

    def activate(buf, row, mean, scale, shift):
        def step(k, _):
            cols = pl.ds(pl.multiple_of(k * CHUNK, CHUNK), CHUNK)
            half = (buf[row, cols].astype(jnp.float32) - mean) * scale + shift
            act[row, cols] = (half + half * jnp.tanh(half)).astype(jnp.bfloat16)
            return 0

        lax.fori_loop(0, width // CHUNK, step, 0, unroll=2)

    def activate_halo(buf, which, mean, scale, shift):
        up, down = halo_copies(buf, which)

        @pl.when(me > 0)
        def _():
            up.wait_send()
            down.wait_recv()
            activate(buf, 0, mean, scale, shift)

        @pl.when(me == 0)
        def _():
            act[0] = jnp.zeros((width, chans), jnp.bfloat16)

        @pl.when(me < n - 1)
        def _():
            down.wait_send()
            up.wait_recv()
            activate(buf, height + 1, mean, scale, shift)

        @pl.when(me == n - 1)
        def _():
            act[height + 1] = jnp.zeros((width, chans), jnp.bfloat16)

    def combine(y):
        size = y[0].shape[0]
        col = lax.rem(lax.broadcasted_iota(jnp.int32, y[0].shape, 0), width)
        total = y[1] + jnp.where(col == 0, 0.0, pltpu.roll(y[0], 1, 0))
        return total + jnp.where(col == width - 1, 0.0, pltpu.roll(y[2], size - 1, 0))

    def mix_weights():
        def step(k, _):
            taps = pl.ds(pl.multiple_of(k * CHUNK, CHUNK), CHUNK)
            for j in range(3):
                ends = 0.5 * (
                    w_out[0, j, taps].astype(jnp.float32) + w_out[2, j, taps].astype(jnp.float32)
                )
                centre = 0.5 * w_out[1, j, taps].astype(jnp.float32)
                w_mix[0, j, taps] = (ends + centre).astype(jnp.bfloat16)
                w_mix[1, j, taps] = (ends - centre).astype(jnp.bfloat16)
            return 0

        lax.fori_loop(0, chans // CHUNK, step, 0)

    def convolve_pair(row, finish):
        def mix(k, _):
            cols = pl.ds(pl.multiple_of(k * CHUNK, CHUNK), CHUNK)
            d = [act[row + i, cols].astype(jnp.float32) for i in range(4)]
            for i, value in enumerate((d[0] - d[2], d[1] + d[2], d[2] - d[1], d[1] - d[3])):
                v_mix[i, cols] = value.astype(jnp.bfloat16)
            return 0

        lax.fori_loop(0, width // CHUNK, mix, 0, unroll=2)

        def step(t, _):
            lanes = pl.ds(pl.multiple_of(t * TILE, TILE), TILE)
            taps = (w_out.at[0], w_mix.at[0], w_mix.at[1], w_out.at[2])
            y = [
                [
                    jnp.dot(v_mix[i], taps[i][j, :, lanes], preferred_element_type=jnp.float32)
                    for j in range(3)
                ]
                for i in range(4)
            ]
            part = [combine(products) for products in y]
            first = part[0] + (part[1] + part[2])
            second = (part[1] - part[2]) - part[3]
            finish(jnp.concatenate([first, second], axis=0), lanes)
            return 0

        lax.fori_loop(0, chans // TILE, step, 0)

    def convolve(rows, weights, finish):
        def step(t, _):
            lanes = pl.ds(pl.multiple_of(t * TILE, TILE), TILE)
            left = jnp.concatenate(
                [jnp.concatenate([act[r + i] for i in range(3)], axis=1) for r in rows], axis=0
            )
            y = [
                jnp.dot(
                    left,
                    weights[:, j, :, lanes].reshape(3 * chans, TILE),
                    preferred_element_type=jnp.float32,
                )
                for j in range(3)
            ]
            total = combine(y)
            finish(total, lanes)
            return 0

        lax.fori_loop(0, chans // TILE, step, 0)

    acc[...] = jnp.zeros_like(acc)
    load.wait()

    def stats_step(k, _):
        cols = pl.ds(pl.multiple_of(k * CHUNK, CHUNK), CHUNK)
        for r in range(height):
            add_stats(img[1 + r, cols].astype(jnp.float32), slice(None))
        return 0

    lax.fori_loop(0, width // CHUNK, stats_step, 0)
    pl.semaphore_wait(barrier, n - 1)
    send_stats(gath_in, 0)
    send_halo(img, 0)
    acc[...] = jnp.zeros_like(acc)

    inner = [(r, r + 1) for r in range(1, height - 1, 2)]
    outer = (0, height - 1)

    load_w_out.wait()
    mix_weights()
    mean, scale = receive_stats(gath_in, 0, gain_in)
    shift = 0.5 * shift_in[...]
    for r in range(1, height + 1):
        activate(img, r, mean, scale, shift)
    load_w_in.wait()

    def keep(rows):
        def finish(total, lanes):
            value = total.astype(jnp.bfloat16)
            add_stats(value.astype(jnp.float32), lanes)
            for k, r in enumerate(rows):
                mid[1 + r, :, lanes] = value[k * width : (k + 1) * width]
        return finish

    for rows in inner:
        convolve(rows, w_in, keep(rows))
    activate_halo(img, 0, mean, scale, shift)
    convolve(outer, w_in, keep(outer))

    send_stats(gath_mid, 1)
    send_halo(mid, 1)
    mean, scale = receive_stats(gath_mid, 1, gain_mid)
    shift = 0.5 * shift_mid[...]
    for r in range(1, height + 1):
        activate(mid, r, mean, scale, shift)

    def give(rows):
        def finish(total, lanes):
            bias = bias_out[:, lanes]
            for k, r in enumerate(rows):
                piece = total[k * width : (k + 1) * width] + bias
                piece = img[1 + r, :, lanes].astype(jnp.float32) + piece
                result[r, :, lanes] = piece.astype(jnp.bfloat16)
        return finish

    def store(r):
        return pltpu.make_async_copy(result.at[r], out.at[r], out_sem.at[r])

    for rows in inner:
        convolve_pair(rows[0], give(rows))
        for r in rows:
            store(r).start()
    activate_halo(mid, 1, mean, scale, shift)
    convolve(outer, w_out, give(outer))
    for r in outer:
        store(r).start()
    for r in range(height):
        store(r).wait()


def local(n, image, gain_in, shift_in, conv_in, gain_mid, shift_mid, conv_out, bias_out):
    height, width, chans = image.shape
    whole = pl.BlockSpec(memory_space=pl.ANY)
    vector = pl.BlockSpec(memory_space=pltpu.VMEM)
    bf16, f32 = jnp.bfloat16, jnp.float32
    rows = 2 * chans // LANES
    return pl.pallas_call(
        functools.partial(kernel, n),
        out_shape=jax.ShapeDtypeStruct(image.shape, image.dtype),
        in_specs=[whole, vector, vector, whole, vector, vector, whole, vector],
        out_specs=whole,
        scratch_shapes=[
            pltpu.VMEM((height + 2, width, chans), bf16),
            pltpu.VMEM((height + 2, width, chans), bf16),
            pltpu.VMEM((height + 2, width, chans), bf16),
            pltpu.VMEM((height, width, chans), bf16),
            pltpu.VMEM(conv_in.shape, bf16),
            pltpu.VMEM(conv_out.shape, bf16),
            pltpu.VMEM((2,) + conv_out.shape[1:], bf16),
            pltpu.VMEM((4, width, chans), bf16),
            pltpu.VMEM((2, 8, chans), f32),
            pltpu.VMEM((n, rows, LANES), f32),
            pltpu.VMEM((n, rows, LANES), f32),
            pltpu.SemaphoreType.DMA((3,)),
            pltpu.SemaphoreType.DMA((height,)),
            pltpu.SemaphoreType.DMA((2, 2)),
            pltpu.SemaphoreType.DMA((2, 2)),
            pltpu.SemaphoreType.DMA((2, n)),
            pltpu.SemaphoreType.DMA((2, n)),
        ],
        compiler_params=pltpu.CompilerParams(
            collective_id=0, has_side_effects=True, vmem_limit_bytes=60 * 1024 * 1024
        ),
    )(image, gain_in[None], shift_in[None], conv_in, gain_mid[None], shift_mid[None], conv_out,
      bias_out[None])


def solution(mesh):
    n = mesh.shape["rows"]
    in_specs = (P(("img", "rows"), None, None), P(), P(), P(), P(), P(), P(), P())
    out_specs = P(("img", "rows"), None, None)
    return jax.shard_map(
        functools.partial(local, n), mesh=mesh, in_specs=in_specs, out_specs=out_specs,
        check_vma=False,
    )
```

profile of v0, /device:TPU:0, one launch (start us, length us, event | category | flops | bytes accessed | tf_op | source)
XLA Modules:
  0.0 32.3 jit_solution(12160278230509236025)
XLA Ops:
  0.0 30.0 %shard_map.82 = bf16[4,256,512]{2,1,0:T(8,128)(2,1)} custom-call(bf16[4,256,512]{2,1,0:T(8,128)(2,1)} %image.1, f32[1,512]{1,0:T(1,128)} %bitcast.5, f32[1,512]{1,0:T(1,128)} %bitcast.6, bf16[3,3,512,512]{3,2,1,0:T(8,128)(2,1)} %conv_in.1, f32[1,512]{1,0:T(1,128)} %bitcast.7, f32[1,512]{1,0:T(1,128)} %bitcast.8, bf16[3,3,512,512]{3,2,1,0:T(8,128)(2,1)} %conv_out.1, ...), custom_call_target="tpu_custom_call" | custom-call | tf_op jit(solution)/shard_map/pallas_call | solution.py:296
  30.0 2.3 %copy.10 = bf16[4,256,512]{2,1,0:T(8,128)(2,1)} copy(bf16[4,256,512]{2,1,0:T(8,128)(2,1)} %shard_map.82) | data formatting | bytes 2097152
where the time goes:
time: 32.5 us; the launch traced here: 32.3 us
  Pallas kernels  30 us (92%)
  local copies, waits for them, and re-layouts  2.26 us (7%)
    pallas_call x1, Pallas kernels, local(): pl.pallas_call(functools.partial(kernel, n), out_shape=jax.ShapeDtypeStru...  30 us
    unnamed x1, local copies, waits for them, and re-layouts  2.26 us

commit v1 on v0

v1 whole, which is shorter than its diff:
```python
import functools

import jax
import jax.numpy as jnp
from jax import lax
from jax.experimental import pallas as pl
from jax.experimental.pallas import tpu as pltpu
from jax.sharding import PartitionSpec as P

GROUPS = 32
LANES = 128
SIDE = 256
UNITS = 2
CHUNK = 32
MESH = pl.DeviceIdType.MESH
BF16, F32 = jnp.bfloat16, jnp.float32


def packed(sums, squares):
    chans = sums.shape[1]
    pieces = [part[:, k : k + LANES] for part in (sums, squares) for k in range(0, chans, LANES)]
    return jnp.concatenate(pieces, axis=0)


def flat(tile):
    return jnp.concatenate([tile[k : k + 1] for k in range(tile.shape[0])], axis=1)


def group_total(tile, size):
    lane = lax.broadcasted_iota(jnp.int32, tile.shape, 1)
    step = 1
    while step < size:
        up = pltpu.roll(tile, step, 1)
        down = pltpu.roll(tile, LANES - step, 1)
        tile = tile + jnp.where((lane & step) != 0, up, down)
        step *= 2
    return tile


def kernel(n, image, gain_in, shift_in, conv_in, gain_mid, shift_mid, conv_out, bias_out, out,
           img, act, mid, w_in, w_out, vec, sums, gath_in, gath_mid,
           img_sem, load_sem, halo_send, halo_recv, stat_send, stat_recv):
    me = lax.axis_index("rows")
    height, width, chans = image.shape
    size = chans // GROUPS
    count = float(height * width * size * n)
    parts = chans // LANES
    depth = chans // SIDE

    order = [0, height - 1] + list(range(1, height - 1))
    loads = {
        r: pltpu.make_async_copy(image.at[r], img.at[1 + r], img_sem.at[r]) for r in order
    }
    for r in order:
        loads[r].start()
    load_w_in = pltpu.make_async_copy(conv_in, w_in, load_sem.at[0])
    load_w_in.start()
    for k, source in enumerate((gain_in, shift_in, gain_mid, shift_mid, bias_out)):
        pltpu.make_async_copy(source, vec.at[pl.ds(k, 1)], load_sem.at[2]).start()
    load_w_out = pltpu.make_async_copy(conv_out, w_out, load_sem.at[1])
    load_w_out.start()

    barrier = pltpu.get_barrier_semaphore()
    for d in range(1, n):
        pl.semaphore_signal(
            barrier, inc=1, device_id={"rows": lax.rem(me + d, n)}, device_id_type=MESH
        )

    def add_stats(value, lanes):
        folded = value.reshape(value.shape[0] // 8, 8, value.shape[1])
        sums[0, :, lanes] += jnp.sum(folded, axis=0)
        sums[1, :, lanes] += jnp.sum(folded * folded, axis=0)

    def stat_copy(gath, which, d):
        return pltpu.make_async_remote_copy(
            src_ref=gath.at[pl.ds(0, 1)],
            dst_ref=gath.at[pl.ds(d, 1)],
            send_sem=stat_send.at[which],
            recv_sem=stat_recv.at[which],
            device_id={"rows": lax.rem(me + d, n)},
            device_id_type=MESH,
        )

    def send_stats(gath, which):
        tile = packed(
            jnp.sum(sums[0], axis=0, keepdims=True), jnp.sum(sums[1], axis=0, keepdims=True)
        )
        tile = group_total(tile, size)
        lane = lax.broadcasted_iota(jnp.int32, tile.shape, 1)
        row = lax.broadcasted_iota(jnp.int32, tile.shape, 0)
        mine = jnp.where(lax.rem(lane, size) == row, tile, 0.0)
        gath[0:1] = jnp.sum(mine, axis=0, keepdims=True)
        for d in range(1, n):
            stat_copy(gath, which, d).start()

    def all_sent(gath, which):
        pltpu.make_async_copy(
            gath.at[pl.ds(1, n - 1)], gath.at[pl.ds(1, n - 1)], stat_send.at[which]
        ).wait()

    def receive_stats(gath, which, gain, shift):
        pltpu.make_async_copy(
            gath.at[pl.ds(1, n - 1)], gath.at[pl.ds(1, n - 1)], stat_recv.at[which]
        ).wait()
        total = jnp.sum(gath[...], axis=0, keepdims=True) / count
        total = jnp.broadcast_to(total, (2 * parts, LANES))
        lane = lax.broadcasted_iota(jnp.int32, total.shape, 1)
        row = lax.broadcasted_iota(jnp.int32, total.shape, 0)
        tile = jnp.take_along_axis(total, lane - lax.rem(lane, size) + row, axis=1)
        mean, square = tile[:parts], tile[parts:]
        variance = jnp.maximum(square - mean * mean, 0.0)
        scale = flat(lax.rsqrt(variance + 1e-06)) * (0.5 * gain)
        return scale, 0.5 * shift - flat(mean) * scale

    def halo_copies(buf, which):
        up = pltpu.make_async_remote_copy(
            src_ref=buf.at[1],
            dst_ref=buf.at[height + 1],
            send_sem=halo_send.at[which, 0],
            recv_sem=halo_recv.at[which, 0],
            device_id={"rows": jnp.maximum(me - 1, 0)},
            device_id_type=MESH,
        )
        down = pltpu.make_async_remote_copy(
            src_ref=buf.at[height],
            dst_ref=buf.at[0],
            send_sem=halo_send.at[which, 1],
            recv_sem=halo_recv.at[which, 1],
            device_id={"rows": jnp.minimum(me + 1, n - 1)},
            device_id_type=MESH,
        )
        return up, down

    def send_halo(buf, which):
        up, down = halo_copies(buf, which)

        @pl.when(me > 0)
        def _():
            up.start()

        @pl.when(me < n - 1)
        def _():
            down.start()

    def wait_halo(buf, which):
        up, down = halo_copies(buf, which)

        @pl.when(me > 0)
        def _():
            up.wait_send()
            down.wait_recv()

        @pl.when(me < n - 1)
        def _():
            down.wait_send()
            up.wait_recv()

    def activate(buf, row, k, scale, shift, inside=None):
        lanes = slice(k * LANES, (k + 1) * LANES)
        half = buf[row, :, lanes].astype(F32) * scale[:, lanes] + shift[:, lanes]
        value = half + half * jnp.tanh(half)
        if inside is not None:
            value = jnp.where(inside, value, 0.0)
        col = lax.broadcasted_iota(jnp.int32, value.shape, 0)
        act[1, row, :, lanes] = value.astype(BF16)
        left = jnp.where(col == 0, 0.0, pltpu.roll(value, 1, 0))
        act[0, row, :, lanes] = left.astype(BF16)
        right = jnp.where(col == width - 1, 0.0, pltpu.roll(value, width - 1, 0))
        act[2, row, :, lanes] = right.astype(BF16)

    def body(*accs):
        acc = [accs[q * height : (q + 1) * height] for q in range(UNITS)]

        zero = jnp.zeros((SIDE, SIDE), BF16)
        for q in range(UNITS):
            for s in range(2):
                pltpu.matmul_acc_lhs(acc[q][0], zero, load_staged_rhs=s)
        for q in range(UNITS):
            for r in range(height):
                pltpu.matmul_pop(acc[q][r])

        def contract(weights, steps, hook=lambda t: None):
            def push(t):
                i, j, k = steps[t][:3]
                for q in range(UNITS):
                    pltpu.matmul_push_rhs(
                        weights[i, j, k * SIDE : (k + 1) * SIDE, q * SIDE : (q + 1) * SIDE],
                        staging_register=t % 2,
                        mxu_index=q,
                    )

            push(0)
            for t, (i, j, k, rows) in enumerate(steps):
                if t + 1 < len(steps):
                    push(t + 1)
                hook(t)
                for m, r in enumerate(rows):
                    left = act[j, r + i, :, k * SIDE : (k + 1) * SIDE]
                    for q in range(UNITS):
                        pltpu.matmul_acc_lhs(
                            acc[q][r], left, load_staged_rhs=t % 2 if m == 0 else None
                        )

        own = [
            (i, j, k, [r for r in range(height) if 1 <= r + i <= height])
            for k in range(depth)
            for i in (1, 0, 2)
            for j in range(3)
        ]
        ends = [
            (i, j, k, [r]) for i, r in ((0, 0), (2, height - 1))
            for k in range(depth) for j in range(3)
        ]
        slabs = SIDE // LANES

        def convolve(buf, which, weights, scale, shift, finish):
            pieces = [
                (r, k) for k in range(parts) for r in range(1, height + 1)
            ]
            early = height * slabs
            for r, k in pieces[:early]:
                activate(buf, r, k, scale, shift)
            rest = pieces[early:]

            def hook(t):
                if rest:
                    r, k = rest.pop(0)
                    activate(buf, r, k, scale, shift)

            contract(weights, own, hook)
            assert not rest
            for r in range(1, height - 1):
                finish(acc, r)
            wait_halo(buf, which)
            for k in range(parts):
                activate(buf, 0, k, scale, shift, me > 0)
                activate(buf, height + 1, k, scale, shift, me < n - 1)
            contract(weights, ends)
            for r in (0, height - 1):
                finish(acc, r)

        sums[...] = jnp.zeros_like(sums)
        for r in order:
            loads[r].wait()

        def stats_step(k, _):
            cols = pl.ds(pl.multiple_of(k * CHUNK, CHUNK), CHUNK)
            for r in range(height):
                add_stats(img[1 + r, cols].astype(F32), slice(None))
            return 0

        lax.fori_loop(0, width // CHUNK, stats_step, 0)
        pl.semaphore_wait(barrier, n - 1)
        send_stats(gath_in, 0)
        send_halo(img, 0)
        sums[...] = jnp.zeros_like(sums)
        load_w_in.wait()
        pltpu.make_async_copy(vec.at[pl.ds(0, 5)], vec.at[pl.ds(0, 5)], load_sem.at[2]).wait()
        scale, shift = receive_stats(gath_in, 0, vec[0:1], vec[1:2])

        def keep(acc, r):
            for q in range(UNITS):
                lanes = slice(q * SIDE, (q + 1) * SIDE)
                value = pltpu.matmul_pop(acc[q][r]).astype(BF16)
                mid[1 + r, :, lanes] = value
                add_stats(value.astype(F32), lanes)

        convolve(img, 0, w_in, scale, shift, keep)
        send_stats(gath_mid, 1)
        send_halo(mid, 1)
        load_w_out.wait()
        scale, shift = receive_stats(gath_mid, 1, vec[2:3], vec[3:4])

        def give(acc, r):
            for q in range(UNITS):
                lanes = slice(q * SIDE, (q + 1) * SIDE)
                value = pltpu.matmul_pop(acc[q][r]) + vec[4:5, lanes]
                out[r, :, lanes] = (img[1 + r, :, lanes].astype(F32) + value).astype(BF16)

        convolve(mid, 1, w_out, scale, shift, give)
        all_sent(gath_in, 0)
        all_sent(gath_mid, 1)

    pl.run_scoped(
        body, *[pltpu.ACC(q)((width, SIDE), F32) for q in range(UNITS) for _ in range(height)]
    )


def pin(x):
    return pltpu.with_memory_space_constraint(x, pltpu.HBM)


def local(n, image, gain_in, shift_in, conv_in, gain_mid, shift_mid, conv_out, bias_out):
    height, width, chans = image.shape
    whole = pl.BlockSpec(memory_space=pltpu.HBM)
    operands = (image, gain_in[None], shift_in[None], conv_in, gain_mid[None], shift_mid[None],
                conv_out, bias_out[None])
    return pl.pallas_call(
        functools.partial(kernel, n),
        out_shape=jax.ShapeDtypeStruct(image.shape, image.dtype),
        in_specs=[whole] * len(operands),
        out_specs=pl.BlockSpec(memory_space=pltpu.VMEM),
        scratch_shapes=[
            pltpu.VMEM((height + 2, width, chans), BF16),
            pltpu.VMEM((3, height + 2, width, chans), BF16),
            pltpu.VMEM((height + 2, width, chans), BF16),
            pltpu.VMEM(conv_in.shape, BF16),
            pltpu.VMEM(conv_out.shape, BF16),
            pltpu.VMEM((8, chans), F32),
            pltpu.VMEM((2, 8, chans), F32),
            pltpu.VMEM((n, LANES), F32),
            pltpu.VMEM((n, LANES), F32),
            pltpu.SemaphoreType.DMA((height,)),
            pltpu.SemaphoreType.DMA((3,)),
            pltpu.SemaphoreType.DMA((2, 2)),
            pltpu.SemaphoreType.DMA((2, 2)),
            pltpu.SemaphoreType.DMA((2,)),
            pltpu.SemaphoreType.DMA((2,)),
        ],
        compiler_params=pltpu.CompilerParams(
            collective_id=0, has_side_effects=True, vmem_limit_bytes=40 * 1024 * 1024
        ),
    )(*[pin(x) for x in operands])


def solution(mesh):
    n = mesh.shape["rows"]
    in_specs = (P(("img", "rows"), None, None), P(), P(), P(), P(), P(), P(), P())
    out_specs = P(("img", "rows"), None, None)
    return jax.shard_map(
        functools.partial(local, n), mesh=mesh, in_specs=in_specs, out_specs=out_specs,
        check_vma=False,
    )
```

time: 32.5 us -> 27.2 us (0.84)
  Pallas kernels: 30 us -> 26.1 us
  local copies, waits for them, and re-layouts: 2.26 us -> 0.97 us
    pallas_call x1, Pallas kernels: 30 us -> 26.1 us  [local(): pl.pallas_call(functools.partial(kernel, n), out_shape=jax.ShapeDtypeStru...]
    unnamed x1, local copies, waits for them, and re-layouts: 2.26 us -> 0.97 us
where the time goes in v1:
time: 27.2 us; the launch traced here: 27.1 us
  Pallas kernels  26.1 us (96%)
  local copies, waits for them, and re-layouts  0.97 us (4%)
    pallas_call x1, Pallas kernels, local(): pl.pallas_call(functools.partial(kernel, n), out_shape=jax.ShapeDtypeStru...  26.1 us
    unnamed x1, local copies, waits for them, and re-layouts  0.97 us

profile of v1, /device:TPU:0, one launch (start us, length us, event | category | flops | bytes accessed | tf_op | source)
XLA Modules:
  0.0 27.1 jit_solution(16094119375789162058)
XLA Ops:
  0.0 26.1 %shard_map.82 = bf16[4,256,512]{2,1,0:T(8,128)(2,1)S(1)} custom-call(bf16[4,256,512]{2,1,0:T(8,128)(2,1)} %image.1, f32[1,512]{1,0:T(1,128)} %bitcast.5, f32[1,512]{1,0:T(1,128)} %bitcast.6, bf16[3,3,512,512]{3,2,1,0:T(8,128)(2,1)} %conv_in.1, f32[1,512]{1,0:T(1,128)} %bitcast.7, f32[1,512]{1,0:T(1,128)} %bitcast.8, bf16[3,3,512,512]{3,2,1,0:T(8,128)(2,1)} %conv_out.1, ...), custom_call_target="tpu_custom_call" | custom-call | tf_op jit(solution)/shard_map/pallas_call | solution.py:298
  26.1 1.0 %copy.10 = bf16[4,256,512]{2,1,0:T(8,128)(2,1)} copy(bf16[4,256,512]{2,1,0:T(8,128)(2,1)S(1)} %shard_map.82) | data formatting | bytes 2097152

commit v2 on v1

v2 whole, which is shorter than its diff:
```python
import functools

import jax
import jax.numpy as jnp
from jax import lax
from jax.experimental import pallas as pl
from jax.experimental.pallas import tpu as pltpu
from jax.sharding import PartitionSpec as P

GROUPS = 32
LANES = 128
SIDE = 256
UNITS = 2
CHUNK = 32
LEAD = 3
TAIL = 3
MESH = pl.DeviceIdType.MESH
BF16, F32 = jnp.bfloat16, jnp.float32


def packed(sums, squares):
    chans = sums.shape[1]
    pieces = [part[:, k : k + LANES] for part in (sums, squares) for k in range(0, chans, LANES)]
    return jnp.concatenate(pieces, axis=0)


def flat(tile):
    return jnp.concatenate([tile[k : k + 1] for k in range(tile.shape[0])], axis=1)


def group_total(tile, size):
    lane = lax.broadcasted_iota(jnp.int32, tile.shape, 1)
    step = 1
    while step < size:
        up = pltpu.roll(tile, step, 1)
        down = pltpu.roll(tile, LANES - step, 1)
        tile = tile + jnp.where((lane & step) != 0, up, down)
        step *= 2
    return tile


def kernel(n, image, gain_in, shift_in, conv_in, gain_mid, shift_mid, conv_out, bias_out, out,
           img, act, mid, w_in, w_out, taps, mixed, part, vec, sums, gath_in, gath_a, gath_b,
           img_sem, load_sem, halo_send, halo_recv, stat_send, stat_recv):
    me = lax.axis_index("rows")
    height, width, chans = image.shape
    size = chans // GROUPS
    count = float(height * width * size * n)
    parts = chans // LANES
    depth = chans // SIDE
    slabs = SIDE // LANES
    share = height // UNITS

    order = [0, height - 1] + list(range(1, height - 1))
    loads = {
        r: pltpu.make_async_copy(image.at[r], img.at[1 + r], img_sem.at[r]) for r in order
    }
    for r in order:
        loads[r].start()
    load_w_in = pltpu.make_async_copy(conv_in, w_in, load_sem.at[0])
    load_w_out = pltpu.make_async_copy(conv_out, w_out, load_sem.at[1])

    barrier = pltpu.get_barrier_semaphore()
    for d in range(1, n):
        pl.semaphore_signal(
            barrier, inc=1, device_id={"rows": lax.rem(me + d, n)}, device_id_type=MESH
        )

    def add_stats(value, lanes):
        folded = value.reshape(value.shape[0] // 8, 8, value.shape[1])
        sums[0, :, lanes] += jnp.sum(folded, axis=0)
        sums[1, :, lanes] += jnp.sum(folded * folded, axis=0)

    def stat_copy(gath, which, d):
        return pltpu.make_async_remote_copy(
            src_ref=gath.at[pl.ds(0, 1)],
            dst_ref=gath.at[pl.ds(d, 1)],
            send_sem=stat_send.at[which],
            recv_sem=stat_recv.at[which],
            device_id={"rows": lax.rem(me + d, n)},
            device_id_type=MESH,
        )

    def prepare_stats(gath, lanes):
        tile = packed(
            jnp.sum(sums[0, :, lanes], axis=0, keepdims=True),
            jnp.sum(sums[1, :, lanes], axis=0, keepdims=True),
        )
        tile = group_total(tile, size)
        lane = lax.broadcasted_iota(jnp.int32, tile.shape, 1)
        row = lax.broadcasted_iota(jnp.int32, tile.shape, 0)
        mine = jnp.where(lax.rem(lane, size) == row, tile, 0.0)
        gath[0:1] = jnp.sum(mine, axis=0, keepdims=True)

    def send_stats(gath, which):
        for d in range(1, n):
            stat_copy(gath, which, d).start()

    def all_sent(gath, which):
        pltpu.make_async_copy(
            gath.at[pl.ds(1, n - 1)], gath.at[pl.ds(1, n - 1)], stat_send.at[which]
        ).wait()

    def receive_stats(gath, which, gain, shift):
        pltpu.make_async_copy(
            gath.at[pl.ds(1, n - 1)], gath.at[pl.ds(1, n - 1)], stat_recv.at[which]
        ).wait()
        pieces = gain.shape[1] // LANES
        total = jnp.sum(gath[...], axis=0, keepdims=True) / count
        total = jnp.broadcast_to(total, (2 * pieces, LANES))
        lane = lax.broadcasted_iota(jnp.int32, total.shape, 1)
        row = lax.broadcasted_iota(jnp.int32, total.shape, 0)
        tile = jnp.take_along_axis(total, lane - lax.rem(lane, size) + row, axis=1)
        mean, square = tile[:pieces], tile[pieces:]
        variance = jnp.maximum(square - mean * mean, 0.0)
        scale = flat(lax.rsqrt(variance + 1e-06)) * (0.5 * gain)
        return scale, 0.5 * shift - flat(mean) * scale

    def halo_copies(buf, which, lanes):
        up = pltpu.make_async_remote_copy(
            src_ref=buf.at[1, :, lanes],
            dst_ref=buf.at[height + 1, :, lanes],
            send_sem=halo_send.at[which, 0],
            recv_sem=halo_recv.at[which, 0],
            device_id={"rows": jnp.maximum(me - 1, 0)},
            device_id_type=MESH,
        )
        down = pltpu.make_async_remote_copy(
            src_ref=buf.at[height, :, lanes],
            dst_ref=buf.at[0, :, lanes],
            send_sem=halo_send.at[which, 1],
            recv_sem=halo_recv.at[which, 1],
            device_id={"rows": jnp.minimum(me + 1, n - 1)},
            device_id_type=MESH,
        )
        return up, down

    def send_halo(buf, which, lanes):
        up, down = halo_copies(buf, which, lanes)

        @pl.when(me > 0)
        def _():
            up.start()

        @pl.when(me < n - 1)
        def _():
            down.start()

    def wait_halo(buf, which, lanes):
        up, down = halo_copies(buf, which, lanes)

        @pl.when(me > 0)
        def _():
            up.wait_send()
            down.wait_recv()

        @pl.when(me < n - 1)
        def _():
            down.wait_send()
            up.wait_recv()

    def activated(buf, row, k, affine):
        lanes = slice(k * LANES, (k + 1) * LANES)
        scale, shift = affine[k]
        half = buf[row, :, lanes].astype(F32) * scale + shift
        value = half + half * jnp.tanh(half)
        if row == 0:
            value = jnp.where(me > 0, value, 0.0)
        if row == height + 1:
            value = jnp.where(me < n - 1, value, 0.0)
        return value

    def store_shifted(target, value, row, lanes):
        col = lax.broadcasted_iota(jnp.int32, value.shape, 0)
        target[1, row, :, lanes] = value.astype(BF16)
        left = jnp.where(col == 0, 0.0, pltpu.roll(value, 1, 0))
        target[0, row, :, lanes] = left.astype(BF16)
        right = jnp.where(col == width - 1, 0.0, pltpu.roll(value, width - 1, 0))
        target[2, row, :, lanes] = right.astype(BF16)

    def activate(buf, row, k, affine):
        value = activated(buf, row, k, affine)
        store_shifted(act, value, row, slice(k * LANES, (k + 1) * LANES))

    def activate_plain(buf, row, k, affine):
        act[1, row, :, k * LANES : (k + 1) * LANES] = activated(buf, row, k, affine).astype(BF16)

    def mix_rows(m, a, b, sign, k, base):
        lanes = slice(k * LANES, (k + 1) * LANES)
        value = act[1, a, :, lanes].astype(F32) + sign * act[1, b, :, lanes].astype(F32)
        store_shifted(mixed, value, m, slice((k - base) * LANES, (k - base + 1) * LANES))

    def mix_taps(base):
        def step(t, _):
            rows = pl.ds(pl.multiple_of(t * CHUNK, CHUNK), CHUNK)
            source = pl.ds(pl.multiple_of(base + t * CHUNK, CHUNK), CHUNK)
            for j in range(3):
                ends = 0.5 * (
                    w_out[0, j, source].astype(F32) + w_out[2, j, source].astype(F32)
                )
                centre = 0.5 * w_out[1, j, source].astype(F32)
                taps[0, j, rows] = (ends + centre).astype(BF16)
                taps[1, j, rows] = (ends - centre).astype(BF16)
            return 0

        lax.fori_loop(0, SIDE // CHUNK, step, 0)

    def body(*accs):
        acc = [accs[q * height : (q + 1) * height] for q in range(UNITS)]

        zero = jnp.zeros((SIDE, SIDE), BF16)
        for q in range(UNITS):
            for s in range(2):
                pltpu.matmul_acc_lhs(acc[q][0], zero, load_staged_rhs=s)
        for q in range(UNITS):
            for r in range(height):
                pltpu.matmul_pop(acc[q][r])

        def contract(steps, hooks=None):
            def push(t):
                for q, (tile, _) in steps[t].items():
                    pltpu.matmul_push_rhs(tile(), staging_register=t % 2, mxu_index=q)

            push(0)
            for t, step in enumerate(steps):
                if t + 1 < len(steps):
                    push(t + 1)
                for hook in (hooks or {}).get(t, []):
                    hook()
                for m in range(height):
                    for q, (_, pairs) in step.items():
                        if m < len(pairs):
                            ref, left = pairs[m]
                            pltpu.matmul_acc_lhs(
                                acc[q][ref], left(), load_staged_rhs=t % 2 if m == 0 else None
                            )

        def tile_of(weights, i, j, k, p):
            return lambda: weights[
                i, j, k * SIDE : (k + 1) * SIDE, p * SIDE : (p + 1) * SIDE
            ]

        def left_of(j, row, k):
            return lambda: act[j, row, :, k * SIDE : (k + 1) * SIDE]

        spots = [(i, j) for j in range(3) for i in (1, 0, 2)]

        def inner(i, rows):
            return [r for r in rows if 1 <= r + i <= height]

        def place(p, r):
            return r // share, p * share + r % share

        def rows_split(w, p, k):
            def entry(i, j, q):
                rows = inner(i, range(q * share, (q + 1) * share))
                pairs = [(place(p, r)[1], left_of(j, r + i, k)) for r in rows]
                return tile_of(w, i, j, k, p), pairs

            own = [{q: entry(i, j, q) for q in range(UNITS)} for i, j in spots]
            ends = [
                {
                    q: (tile_of(w, i, j, k, p), [(place(p, r)[1], left_of(j, r + i, k))])
                    for q, i, r in ((0, 0, 0), (UNITS - 1, 2, height - 1))
                }
                for j in range(3)
            ]
            return own, ends

        def rows_first(w, p, k):
            queues = []
            for q in range(UNITS):
                rows = list(range(q * share, (q + 1) * share))
                inputs = range(1, height + 1) if q == 0 else range(height, 0, -1)
                queues.append([
                    (tile_of(w, x - r, j, k, p), [(place(p, r)[1], left_of(j, x, k))])
                    for x in inputs
                    for j in range(3)
                    for r in (rows if q == 0 else rows[::-1])
                    if 0 <= x - r <= 2
                ])
            return [dict(enumerate(step)) for step in zip(*queues, strict=True)]

        def chans_split(w, k):
            own = [
                {
                    q: (tile_of(w, i, j, k, q),
                        [(r, left_of(j, r + i, k)) for r in inner(i, range(height))])
                    for q in range(UNITS)
                }
                for i, j in spots
            ]
            ends = [
                {q: (tile_of(w, i, j, k, q), [(r, left_of(j, r + i, k))]) for q in range(UNITS)}
                for i, r in ((0, 0), (2, height - 1))
                for j in range(3)
            ]
            return own, ends

        def spread(hooks, first, last):
            assert first < last
            steps = range(first, last)
            plan = {t: [] for t in steps}
            for m, hook in enumerate(hooks):
                plan[first + m * len(steps) // len(hooks)].append(hook)
            return plan

        def lanes_of(p):
            return slice(p * SIDE, (p + 1) * SIDE)

        def rows_act(buf, rows, ks, affine):
            return [
                functools.partial(activate, buf, r, k, affine) for k in ks for r in rows
            ]

        def affine_of(pair, first=0):
            scale, shift = pair
            return {
                first + k: (scale[:, k * LANES : (k + 1) * LANES], shift[:, k * LANES : (k + 1) * LANES])
                for k in range(scale.shape[1] // LANES)
            }

        mine = range(1, height + 1)
        halo = (0, height + 1)

        sums[...] = jnp.zeros_like(sums)
        def stats_step(r, k, _):
            cols = pl.ds(pl.multiple_of(k * CHUNK, CHUNK), CHUNK)
            add_stats(img[1 + r, cols].astype(F32), slice(None))
            return 0

        for r in order:
            loads[r].wait()
            if r == order[-1]:
                for k, source in enumerate((gain_in, shift_in, gain_mid, shift_mid, bias_out)):
                    pltpu.make_async_copy(source, vec.at[pl.ds(k, 1)], load_sem.at[2]).start()
                load_w_in.start()
                load_w_out.start()
            lax.fori_loop(0, width // CHUNK, functools.partial(stats_step, r), 0)
        prepare_stats(gath_in, slice(None))
        pl.semaphore_wait(barrier, n - 1)
        send_stats(gath_in, 0)
        send_halo(img, 0, slice(None))
        sums[...] = jnp.zeros_like(sums)
        load_w_in.wait()
        load_w_out.wait()
        mix_taps(SIDE)
        pltpu.make_async_copy(vec.at[pl.ds(0, 5)], vec.at[pl.ds(0, 5)], load_sem.at[2]).wait()
        affine = affine_of(receive_stats(gath_in, 0, vec[0:1], vec[1:2]))

        def keep(p, r):
            lanes = lanes_of(p)
            q, ref = place(p, r)
            value = pltpu.matmul_pop(acc[q][ref]).astype(BF16)
            mid[1 + r, :, lanes] = value
            add_stats(value.astype(F32), lanes)

        middle = range(1, height - 1)
        outer = (0, height - 1)

        def kept(p, rows):
            return [functools.partial(keep, p, r) for r in rows]

        def both(p):
            first = [rows_split(w_in, p, k) for k in range(depth)]
            return [sum((pair[m] for pair in first), []) for m in range(2)]

        own_b, ends_b = both(1)
        _, ends_a = both(0)
        near = (1, height)
        far = [r for r in mine if r not in near]
        for hook in rows_act(img, near, range(slabs), affine):
            hook()
        start = rows_first(w_in, 0, 0)
        plan = spread(rows_act(img, far, range(slabs), affine), 0, 4)
        plan.update(spread(rows_act(img, mine, range(slabs, parts), affine), 4, len(start)))
        contract(start, plan)
        later = sum((rows_split(w_in, 0, k)[0] for k in range(1, depth)), [])
        contract(later[:-TAIL])
        wait_halo(img, 0, slice(None))
        contract(later[-TAIL:], spread(rows_act(img, halo, range(parts), affine), 0, TAIL))
        contract(ends_a, spread(kept(0, middle), 2, len(ends_a)))
        contract(
            own_b[:LEAD],
            spread(kept(0, outer) + [functools.partial(prepare_stats, gath_a, lanes_of(0))], 0, LEAD),
        )
        send_stats(gath_a, 1)
        send_halo(mid, 1, lanes_of(0))
        contract(own_b[LEAD:])
        contract(ends_b, spread(kept(1, middle), 1, len(ends_b)))
        for hook in kept(1, outer):
            hook()
        prepare_stats(gath_b, lanes_of(1))
        send_stats(gath_b, 2)
        send_halo(mid, 2, lanes_of(1))

        def give(r, ref):
            for q in range(UNITS):
                lanes = lanes_of(q)
                value = pltpu.matmul_pop(acc[q][ref]) + (part[r, :, lanes] + vec[4:5, lanes])
                out[r, :, lanes] = (img[1 + r, :, lanes].astype(F32) + value).astype(BF16)

        def save(r):
            for q in range(UNITS):
                part[r, :, lanes_of(q)] = pltpu.matmul_pop(acc[q][r])

        def fold(r, first, second, q):
            lanes = lanes_of(q)
            a, b = pltpu.matmul_pop(acc[q][first]), pltpu.matmul_pop(acc[q][second])
            part[r, :, lanes] += a + b
            part[r + 1, :, lanes] += a - b

        def ready(p, gath):
            lanes = lanes_of(p)
            pair = receive_stats(gath, 1 + p, vec[2:3, lanes], vec[3:4, lanes])
            return affine_of(pair, p * slabs)

        affine = ready(0, gath_a)
        here = range(slabs)
        for hook in rows_act(mid, mine, here, affine):
            hook()
        steps, last = chans_split(w_out, 0)
        contract(steps[:-TAIL])
        wait_halo(mid, 1, lanes_of(0))
        contract(steps[-TAIL:], spread(rows_act(mid, halo, here, affine), 0, TAIL))
        contract(last, spread([functools.partial(save, r) for r in middle], 2, len(last)))
        for r in outer:
            save(r)

        affine = ready(1, gath_b)
        here = range(slabs, 2 * slabs)

        def plain(r):
            return [functools.partial(activate_plain, mid, r, k, affine) for k in here]

        def pair_mix(m, a, b, sign):
            return [functools.partial(mix_rows, m, a, b, sign, k, slabs) for k in here]

        combos = [
            (1, 2, 1.0, 0, 0), (2, 1, -1.0, 1, 1), (3, 1, -1.0, None, 2),
            (3, 4, 1.0, 0, 3), (4, 3, -1.0, 1, 0), (2, 4, -1.0, None, 1),
            (0, 2, -1.0, None, 2), (5, 3, -1.0, None, 3),
        ]
        sides = {2: 2, 5: 0, 6: 0, 7: 2}

        def mixing(m):
            return pair_mix(m, *combos[m][:3])

        def product(m):
            kind, ref = combos[m][3:]

            def entry(j, q):
                columns = slice(q * SIDE, (q + 1) * SIDE)
                if kind is None:
                    tile = tile_of(w_out, sides[m], j, 1, q)
                else:
                    tile = lambda: taps[kind, j, :, columns]
                return tile, [(ref, lambda: mixed[j, m])]

            return [{q: entry(j, q) for q in range(UNITS)} for j in range(3)]

        for hook in plain(1) + plain(2) + mixing(0):
            hook()
        steps = sum((product(m) for m in range(8)), [])
        plan = spread(mixing(1) + plain(3), 0, 3)
        plan.update(spread(mixing(2) + plain(4), 3, 6))
        plan.update(spread(
            mixing(3) + [functools.partial(fold, 0, 0, 1, q) for q in range(UNITS)], 6, 10
        ))
        plan.update(spread(mixing(4) + [functools.partial(give, 1, 2)], 10, 13))
        plan.update(spread(mixing(5), 13, 15))
        contract(steps[:15], plan)
        wait_halo(mid, 2, lanes_of(1))
        plan = spread(plain(0) + mixing(6), 0, 2)
        plan.update(spread(
            plain(5) + [functools.partial(fold, 2, 3, 0, q) for q in range(UNITS)], 2, 4
        ))
        plan.update(spread(mixing(7) + [functools.partial(give, 2, 1)], 4, 7))
        plan.update({8: [functools.partial(give, 0, 2)]})
        contract(steps[15:], plan)
        give(height - 1, 3)
        all_sent(gath_in, 0)
        all_sent(gath_a, 1)
        all_sent(gath_b, 2)

    pl.run_scoped(
        body, *[pltpu.ACC(q)((width, SIDE), F32) for q in range(UNITS) for _ in range(height)]
    )


def pin(x):
    return pltpu.with_memory_space_constraint(x, pltpu.HBM)


def local(n, image, gain_in, shift_in, conv_in, gain_mid, shift_mid, conv_out, bias_out):
    height, width, chans = image.shape
    whole = pl.BlockSpec(memory_space=pltpu.HBM)
    operands = (image, gain_in[None], shift_in[None], conv_in, gain_mid[None], shift_mid[None],
                conv_out, bias_out[None])
    return pl.pallas_call(
        functools.partial(kernel, n),
        out_shape=jax.ShapeDtypeStruct(image.shape, image.dtype),
        in_specs=[whole] * len(operands),
        out_specs=pl.BlockSpec(memory_space=pltpu.VMEM),
        scratch_shapes=[
            pltpu.VMEM((height + 2, width, chans), BF16),
            pltpu.VMEM((3, height + 2, width, chans), BF16),
            pltpu.VMEM((height + 2, width, chans), BF16),
            pltpu.VMEM(conv_in.shape, BF16),
            pltpu.VMEM(conv_out.shape, BF16),
            pltpu.VMEM((2, 3, SIDE, chans), BF16),
            pltpu.VMEM((3, 8, width, SIDE), BF16),
            pltpu.VMEM((height, width, chans), F32),
            pltpu.VMEM((8, chans), F32),
            pltpu.VMEM((2, 8, chans), F32),
            pltpu.VMEM((n, LANES), F32),
            pltpu.VMEM((n, LANES), F32),
            pltpu.VMEM((n, LANES), F32),
            pltpu.SemaphoreType.DMA((height,)),
            pltpu.SemaphoreType.DMA((3,)),
            pltpu.SemaphoreType.DMA((3, 2)),
            pltpu.SemaphoreType.DMA((3, 2)),
            pltpu.SemaphoreType.DMA((3,)),
            pltpu.SemaphoreType.DMA((3,)),
        ],
        compiler_params=pltpu.CompilerParams(
            collective_id=0, has_side_effects=True, vmem_limit_bytes=44 * 1024 * 1024
        ),
    )(*[pin(x) for x in operands])


def solution(mesh):
    n = mesh.shape["rows"]
    in_specs = (P(("img", "rows"), None, None), P(), P(), P(), P(), P(), P(), P())
    out_specs = P(("img", "rows"), None, None)
    return jax.shard_map(
        functools.partial(local, n), mesh=mesh, in_specs=in_specs, out_specs=out_specs,
        check_vma=False,
    )
```

time: 27.2 us -> 25.1 us (0.923)
  Pallas kernels: 26.1 us -> 24 us
    pallas_call x1, Pallas kernels: 26.1 us -> 24 us  [local(): pl.pallas_call(functools.partial(kernel, n), out_shape=jax.ShapeDtypeStru...]
where the time goes in v2:
time: 25.1 us; the launch traced here: 25 us
  Pallas kernels  24 us (96%)
  local copies, waits for them, and re-layouts  0.97 us (4%)
    pallas_call x1, Pallas kernels, local(): pl.pallas_call(functools.partial(kernel, n), out_shape=jax.ShapeDtypeStru...  24 us
    unnamed x1, local copies, waits for them, and re-layouts  0.97 us

profile of v2, /device:TPU:0, one launch (start us, length us, event | category | flops | bytes accessed | tf_op | source)
XLA Modules:
  0.0 25.0 jit_solution(2808263159205351129)
XLA Ops:
  0.0 24.0 %shard_map.82 = bf16[4,256,512]{2,1,0:T(8,128)(2,1)S(1)} custom-call(bf16[4,256,512]{2,1,0:T(8,128)(2,1)} %image.1, f32[1,512]{1,0:T(1,128)} %bitcast.5, f32[1,512]{1,0:T(1,128)} %bitcast.6, bf16[3,3,512,512]{3,2,1,0:T(8,128)(2,1)} %conv_in.1, f32[1,512]{1,0:T(1,128)} %bitcast.7, f32[1,512]{1,0:T(1,128)} %bitcast.8, bf16[3,3,512,512]{3,2,1,0:T(8,128)(2,1)} %conv_out.1, ...), custom_call_target="tpu_custom_call" | custom-call | tf_op jit(solution)/shard_map/pallas_call | solution.py:500
  24.0 1.0 %copy.10 = bf16[4,256,512]{2,1,0:T(8,128)(2,1)} copy(bf16[4,256,512]{2,1,0:T(8,128)(2,1)S(1)} %shard_map.82) | data formatting | bytes 2097152

commit v3 on v2

--- a/solution.py
+++ b/solution.py
@@ -12,8 +12,10 @@
 SIDE = 256
 UNITS = 2
 CHUNK = 32
-LEAD = 3
-TAIL = 3
+PAD = 8
+LEAD = 4
+SOAK = 1
+DRAIN = 2
 MESH = pl.DeviceIdType.MESH
 BF16, F32 = jnp.bfloat16, jnp.float32
 
@@ -32,10 +34,17 @@
     lane = lax.broadcasted_iota(jnp.int32, tile.shape, 1)
     step = 1
     while step < size:
-        up = pltpu.roll(tile, step, 1)
-        down = pltpu.roll(tile, LANES - step, 1)
-        tile = tile + jnp.where((lane & step) != 0, up, down)
-        step *= 2
+        far = min(4, size // step)
+        place = (lane // step) % far
+        turned = {d: pltpu.roll(tile, (d * step) % LANES, 1) for d in range(1 - far, far) if d}
+        total = tile
+        for p in range(1, far):
+            other = turned[p]
+            for d in range(p):
+                other = jnp.where(place == d, turned[p - far], other)
+            total = total + other
+        tile = total
+        step *= far
     return tile
 
 
@@ -170,37 +179,34 @@
             value = jnp.where(me < n - 1, value, 0.0)
         return value
 
-    def store_shifted(target, value, row, lanes):
-        col = lax.broadcasted_iota(jnp.int32, value.shape, 0)
-        target[1, row, :, lanes] = value.astype(BF16)
-        left = jnp.where(col == 0, 0.0, pltpu.roll(value, 1, 0))
-        target[0, row, :, lanes] = left.astype(BF16)
-        right = jnp.where(col == width - 1, 0.0, pltpu.roll(value, width - 1, 0))
-        target[2, row, :, lanes] = right.astype(BF16)
+    inside = pl.ds(PAD, width)
 
     def activate(buf, row, k, affine):
-        value = activated(buf, row, k, affine)
-        store_shifted(act, value, row, slice(k * LANES, (k + 1) * LANES))
-
-    def activate_plain(buf, row, k, affine):
-        act[1, row, :, k * LANES : (k + 1) * LANES] = activated(buf, row, k, affine).astype(BF16)
+        act[row, k, inside] = activated(buf, row, k, affine)
+
+    def activate_round(buf, row, k, affine):
+        act[row, k, inside] = activated(buf, row, k, affine).astype(BF16).astype(F32)
 
     def mix_rows(m, a, b, sign, k, base):
-        lanes = slice(k * LANES, (k + 1) * LANES)
-        value = act[1, a, :, lanes].astype(F32) + sign * act[1, b, :, lanes].astype(F32)
-        store_shifted(mixed, value, m, slice((k - base) * LANES, (k - base + 1) * LANES))
-
-    def mix_taps(base):
+        mixed[m, k - base, inside] = act[a, k, inside] + sign * act[b, k, inside]
+
+    def shifted(buf, row, j, k):
+        cols = pl.ds(PAD + j - 1, width)
+        return jnp.concatenate(
+            [buf[row, k * slabs + m, cols] for m in range(slabs)], axis=1
+        )
+
+    def mix_taps(p):
         def step(t, _):
             rows = pl.ds(pl.multiple_of(t * CHUNK, CHUNK), CHUNK)
-            source = pl.ds(pl.multiple_of(base + t * CHUNK, CHUNK), CHUNK)
+            source = pl.ds(pl.multiple_of(p * SIDE + t * CHUNK, CHUNK), CHUNK)
             for j in range(3):
                 ends = 0.5 * (
                     w_out[0, j, source].astype(F32) + w_out[2, j, source].astype(F32)
                 )
                 centre = 0.5 * w_out[1, j, source].astype(F32)
-                taps[0, j, rows] = (ends + centre).astype(BF16)
-                taps[1, j, rows] = (ends - centre).astype(BF16)
+                taps[p, 0, j, rows] = (ends + centre).astype(BF16)
+                taps[p, 1, j, rows] = (ends - centre).astype(BF16)
             return 0
 
         lax.fori_loop(0, SIDE // CHUNK, step, 0)
@@ -241,7 +247,7 @@
             ]
 
         def left_of(j, row, k):
-            return lambda: act[j, row, :, k * SIDE : (k + 1) * SIDE]
+            return lambda: shifted(act, row, j, k)
 
         spots = [(i, j) for j in range(3) for i in (1, 0, 2)]
 
@@ -281,22 +287,6 @@
                 ])
             return [dict(enumerate(step)) for step in zip(*queues, strict=True)]
 
-        def chans_split(w, k):
-            own = [
-                {
-                    q: (tile_of(w, i, j, k, q),
-                        [(r, left_of(j, r + i, k)) for r in inner(i, range(height))])
-                    for q in range(UNITS)
-                }
-                for i, j in spots
-            ]
-            ends = [
-                {q: (tile_of(w, i, j, k, q), [(r, left_of(j, r + i, k))]) for q in range(UNITS)}
-                for i, r in ((0, 0), (2, height - 1))
-                for j in range(3)
-            ]
-            return own, ends
-
         def spread(hooks, first, last):
             assert first < last
             steps = range(first, last)
@@ -324,6 +314,11 @@
         halo = (0, height + 1)
 
         sums[...] = jnp.zeros_like(sums)
+        for buf in (act, mixed):
+            edge = jnp.zeros(buf.shape[:2] + (PAD, LANES), F32)
+            buf[:, :, 0:PAD] = edge
+            buf[:, :, PAD + width : 2 * PAD + width] = edge
+
         def stats_step(r, k, _):
             cols = pl.ds(pl.multiple_of(k * CHUNK, CHUNK), CHUNK)
             add_stats(img[1 + r, cols].astype(F32), slice(None))
@@ -344,7 +339,8 @@
         sums[...] = jnp.zeros_like(sums)
         load_w_in.wait()
         load_w_out.wait()
-        mix_taps(SIDE)
+        for p in range(depth):
+            mix_taps(p)
         pltpu.make_async_copy(vec.at[pl.ds(0, 5)], vec.at[pl.ds(0, 5)], load_sem.at[2]).wait()
         affine = affine_of(receive_stats(gath_in, 0, vec[0:1], vec[1:2]))
 
@@ -376,17 +372,25 @@
         plan.update(spread(rows_act(img, mine, range(slabs, parts), affine), 4, len(start)))
         contract(start, plan)
         later = sum((rows_split(w_in, 0, k)[0] for k in range(1, depth)), [])
-        contract(later[:-TAIL])
+        contract(later)
+        contract(own_b[:LEAD])
         wait_halo(img, 0, slice(None))
-        contract(later[-TAIL:], spread(rows_act(img, halo, range(parts), affine), 0, TAIL))
-        contract(ends_a, spread(kept(0, middle), 2, len(ends_a)))
         contract(
-            own_b[:LEAD],
-            spread(kept(0, outer) + [functools.partial(prepare_stats, gath_a, lanes_of(0))], 0, LEAD),
+            own_b[LEAD : LEAD + SOAK],
+            spread(rows_act(img, halo, range(slabs), affine), 0, SOAK),
+        )
+        plan = spread(rows_act(img, halo, range(slabs, parts), affine), 0, 2)
+        plan.update(spread(kept(0, middle), 3, len(ends_a)))
+        contract(ends_a, plan)
+        contract(
+            own_b[LEAD + SOAK : LEAD + SOAK + DRAIN],
+            spread(
+                kept(0, outer) + [functools.partial(prepare_stats, gath_a, lanes_of(0))], 0, DRAIN
+            ),
         )
         send_stats(gath_a, 1)
         send_halo(mid, 1, lanes_of(0))
-        contract(own_b[LEAD:])
+        contract(own_b[LEAD + SOAK + DRAIN :])
         contract(ends_b, spread(kept(1, middle), 1, len(ends_b)))
         for hook in kept(1, outer):
             hook()
@@ -400,41 +404,19 @@
                 value = pltpu.matmul_pop(acc[q][ref]) + (part[r, :, lanes] + vec[4:5, lanes])
                 out[r, :, lanes] = (img[1 + r, :, lanes].astype(F32) + value).astype(BF16)
 
-        def save(r):
-            for q in range(UNITS):
-                part[r, :, lanes_of(q)] = pltpu.matmul_pop(acc[q][r])
-
-        def fold(r, first, second, q):
+        def fold(p, r, first, second, q):
             lanes = lanes_of(q)
             a, b = pltpu.matmul_pop(acc[q][first]), pltpu.matmul_pop(acc[q][second])
-            part[r, :, lanes] += a + b
-            part[r + 1, :, lanes] += a - b
-
-        def ready(p, gath):
-            lanes = lanes_of(p)
-            pair = receive_stats(gath, 1 + p, vec[2:3, lanes], vec[3:4, lanes])
-            return affine_of(pair, p * slabs)
-
-        affine = ready(0, gath_a)
-        here = range(slabs)
-        for hook in rows_act(mid, mine, here, affine):
-            hook()
-        steps, last = chans_split(w_out, 0)
-        contract(steps[:-TAIL])
-        wait_halo(mid, 1, lanes_of(0))
-        contract(steps[-TAIL:], spread(rows_act(mid, halo, here, affine), 0, TAIL))
-        contract(last, spread([functools.partial(save, r) for r in middle], 2, len(last)))
-        for r in outer:
-            save(r)
-
-        affine = ready(1, gath_b)
-        here = range(slabs, 2 * slabs)
-
-        def plain(r):
-            return [functools.partial(activate_plain, mid, r, k, affine) for k in here]
-
-        def pair_mix(m, a, b, sign):
-            return [functools.partial(mix_rows, m, a, b, sign, k, slabs) for k in here]
+            if p == 0:
+                part[r, :, lanes] = a + b
+                part[r + 1, :, lanes] = a - b
+            else:
+                part[r, :, lanes] += a + b
+                part[r + 1, :, lanes] += a - b
+
+        def save(r, ref):
+            for q in range(UNITS):
+                part[r, :, lanes_of(q)] += pltpu.matmul_pop(acc[q][ref])
 
         combos = [
             (1, 2, 1.0, 0, 0), (2, 1, -1.0, 1, 1), (3, 1, -1.0, None, 2),
@@ -443,42 +425,66 @@
         ]
         sides = {2: 2, 5: 0, 6: 0, 7: 2}
 
-        def mixing(m):
-            return pair_mix(m, *combos[m][:3])
-
-        def product(m):
+        def product(m, p):
             kind, ref = combos[m][3:]
 
             def entry(j, q):
                 columns = slice(q * SIDE, (q + 1) * SIDE)
                 if kind is None:
-                    tile = tile_of(w_out, sides[m], j, 1, q)
+                    tile = tile_of(w_out, sides[m], j, p, q)
                 else:
-                    tile = lambda: taps[kind, j, :, columns]
-                return tile, [(ref, lambda: mixed[j, m])]
+                    tile = lambda: taps[p, kind, j, :, columns]
+                return tile, [(ref, lambda: shifted(mixed, m, j, 0))]
 
             return [{q: entry(j, q) for q in range(UNITS)} for j in range(3)]
 
-        for hook in plain(1) + plain(2) + mixing(0):
+        def second(p, affine):
+            here = range(p * slabs, (p + 1) * slabs)
+            put = save if p < depth - 1 else give
+
+            def plain(r):
+                return [functools.partial(activate_round, mid, r, k, affine) for k in here]
+
+            def mixing(m):
+                return [
+                    functools.partial(mix_rows, m, *combos[m][:3], k, p * slabs) for k in here
+                ]
+
+            def folding(r, first, other):
+                return [functools.partial(fold, p, r, first, other, q) for q in range(UNITS)]
+
+            steps = sum((product(m, p) for m in range(8)), [])
+            early = spread(mixing(1) + plain(3), 0, 3)
+            early.update(spread(mixing(2) + plain(4), 3, 6))
+            early.update(spread(mixing(3) + folding(0, 0, 1), 6, 10))
+            early.update(spread(mixing(4) + [functools.partial(put, 1, 2)], 10, 13))
+            early.update(spread(mixing(5), 13, 15))
+            late = spread(plain(0) + mixing(6), 0, 2)
+            late.update(spread(plain(5) + folding(2, 3, 0), 2, 4))
+            late.update(spread(mixing(7) + [functools.partial(put, 2, 1)], 4, 7))
+            late.update({8: [functools.partial(put, 0, 2)]})
+            opening = plain(1) + plain(2) + mixing(0)
+            return opening, steps[:15], early, steps[15:], late, functools.partial(put, height - 1, 3)
+
+        def ready(p, gath):
+            lanes = lanes_of(p)
+            pair = receive_stats(gath, 1 + p, vec[2:3, lanes], vec[3:4, lanes])
+            return second(p, affine_of(pair, p * slabs))
+
+        opening, steps, plan, rest, rest_plan, closing = ready(0, gath_a)
+        for hook in opening:
             hook()
-        steps = sum((product(m) for m in range(8)), [])
-        plan = spread(mixing(1) + plain(3), 0, 3)
-        plan.update(spread(mixing(2) + plain(4), 3, 6))
-        plan.update(spread(
-            mixing(3) + [functools.partial(fold, 0, 0, 1, q) for q in range(UNITS)], 6, 10
-        ))
-        plan.update(spread(mixing(4) + [functools.partial(give, 1, 2)], 10, 13))
-        plan.update(spread(mixing(5), 13, 15))
-        contract(steps[:15], plan)
+        contract(steps, plan)
+        wait_halo(mid, 1, lanes_of(0))
+        contract(rest, rest_plan)
+        opening, steps, plan, last, last_plan, final = ready(1, gath_b)
+        for hook in opening:
+            hook()
+        plan[2] = plan[2] + [closing]
+        contract(steps, plan)
         wait_halo(mid, 2, lanes_of(1))
-        plan = spread(plain(0) + mixing(6), 0, 2)
-        plan.update(spread(
-            plain(5) + [functools.partial(fold, 2, 3, 0, q) for q in range(UNITS)], 2, 4
-        ))
-        plan.update(spread(mixing(7) + [functools.partial(give, 2, 1)], 4, 7))
-        plan.update({8: [functools.partial(give, 0, 2)]})
-        contract(steps[15:], plan)
-        give(height - 1, 3)
+        contract(last, last_plan)
+        final()
         all_sent(gath_in, 0)
         all_sent(gath_a, 1)
         all_sent(gath_b, 2)
@@ -504,12 +510,12 @@
         out_specs=pl.BlockSpec(memory_space=pltpu.VMEM),
         scratch_shapes=[
             pltpu.VMEM((height + 2, width, chans), BF16),
-            pltpu.VMEM((3, height + 2, width, chans), BF16),
+            pltpu.VMEM((height + 2, chans // LANES, width + 2 * PAD, LANES), F32),
             pltpu.VMEM((height + 2, width, chans), BF16),
             pltpu.VMEM(conv_in.shape, BF16),
             pltpu.VMEM(conv_out.shape, BF16),
-            pltpu.VMEM((2, 3, SIDE, chans), BF16),
-            pltpu.VMEM((3, 8, width, SIDE), BF16),
+            pltpu.VMEM((chans // SIDE, 2, 3, SIDE, chans), BF16),
+            pltpu.VMEM((8, SIDE // LANES, width + 2 * PAD, LANES), F32),
             pltpu.VMEM((height, width, chans), F32),
             pltpu.VMEM((8, chans), F32),
             pltpu.VMEM((2, 8, chans), F32),

time: 25.1 us -> 23.1 us (0.920)
  Pallas kernels: 24 us -> 22 us
    pallas_call x1, Pallas kernels: 24 us -> 22 us  [local(): pl.pallas_call(functools.partial(kernel, n), out_shape=jax.ShapeDtypeStru...]
where the time goes in v3:
time: 23.1 us; the launch traced here: 23 us
  Pallas kernels  22 us (95%)
  local copies, waits for them, and re-layouts  0.97 us (4%)
    pallas_call x1, Pallas kernels, local(): pl.pallas_call(functools.partial(kernel, n), out_shape=jax.ShapeDtypeStru...  22 us
    unnamed x1, local copies, waits for them, and re-layouts  0.97 us

profile of v3, /device:TPU:0, one launch (start us, length us, event | category | flops | bytes accessed | tf_op | source)
XLA Modules:
  0.0 23.0 jit_solution(1540485414701836230)
XLA Ops:
  0.0 22.0 %shard_map.82 = bf16[4,256,512]{2,1,0:T(8,128)(2,1)S(1)} custom-call(bf16[4,256,512]{2,1,0:T(8,128)(2,1)} %image.1, f32[1,512]{1,0:T(1,128)} %bitcast.5, f32[1,512]{1,0:T(1,128)} %bitcast.6, bf16[3,3,512,512]{3,2,1,0:T(8,128)(2,1)} %conv_in.1, f32[1,512]{1,0:T(1,128)} %bitcast.7, f32[1,512]{1,0:T(1,128)} %bitcast.8, bf16[3,3,512,512]{3,2,1,0:T(8,128)(2,1)} %conv_out.1, ...), custom_call_target="tpu_custom_call" | custom-call | tf_op jit(solution)/shard_map/pallas_call | solution.py:506
  22.0 1.0 %copy.10 = bf16[4,256,512]{2,1,0:T(8,128)(2,1)} copy(bf16[4,256,512]{2,1,0:T(8,128)(2,1)S(1)} %shard_map.82) | data formatting | bytes 2097152

commit v4 on v3

--- a/solution.py
+++ b/solution.py
@@ -13,9 +13,10 @@
 UNITS = 2
 CHUNK = 32
 PAD = 8
-LEAD = 4
+LEAD = 1
+TURN = 5
 SOAK = 1
-DRAIN = 2
+DRAIN = 3
 MESH = pl.DeviceIdType.MESH
 BF16, F32 = jnp.bfloat16, jnp.float32
 
@@ -49,7 +50,7 @@
 
 
 def kernel(n, image, gain_in, shift_in, conv_in, gain_mid, shift_mid, conv_out, bias_out, out,
-           img, act, mid, w_in, w_out, taps, mixed, part, vec, sums, gath_in, gath_a, gath_b,
+           img, act, mid, w_in, w_out, taps_in, taps, mixed, part, vec, sums, gath_in, gath_a, gath_b,
            img_sem, load_sem, halo_send, halo_recv, stat_send, stat_recv):
     me = lax.axis_index("rows")
     height, width, chans = image.shape
@@ -102,7 +103,7 @@
         gath[0:1] = jnp.sum(mine, axis=0, keepdims=True)
 
     def send_stats(gath, which):
-        for d in range(1, n):
+        for d in sorted(range(1, n), key=lambda d: min(d, n - d)):
             stat_copy(gath, which, d).start()
 
     def all_sent(gath, which):
@@ -115,7 +116,7 @@
             gath.at[pl.ds(1, n - 1)], gath.at[pl.ds(1, n - 1)], stat_recv.at[which]
         ).wait()
         pieces = gain.shape[1] // LANES
-        total = jnp.sum(gath[...], axis=0, keepdims=True) / count
+        total = jnp.sum(gath[...], axis=0, keepdims=True) * (1.0 / count)
         total = jnp.broadcast_to(total, (2 * pieces, LANES))
         lane = lax.broadcasted_iota(jnp.int32, total.shape, 1)
         row = lax.broadcasted_iota(jnp.int32, total.shape, 0)
@@ -190,11 +191,29 @@
     def mix_rows(m, a, b, sign, k, base):
         mixed[m, k - base, inside] = act[a, k, inside] + sign * act[b, k, inside]
 
+    def mix_rounded(m, a, b, sign, k):
+        first = act[a, k, inside].astype(BF16).astype(F32)
+        mixed[m, k, inside] = first + sign * act[b, k, inside].astype(BF16).astype(F32)
+
     def shifted(buf, row, j, k):
         cols = pl.ds(PAD + j - 1, width)
         return jnp.concatenate(
             [buf[row, k * slabs + m, cols] for m in range(slabs)], axis=1
         )
+
+    def mix_taps_in(columns):
+        def step(t, _):
+            rows = pl.ds(pl.multiple_of(t * CHUNK, CHUNK), CHUNK)
+            for j in range(3):
+                ends = 0.5 * (
+                    w_in[0, j, rows, columns].astype(F32) + w_in[2, j, rows, columns].astype(F32)
+                )
+                centre = 0.5 * w_in[1, j, rows, columns].astype(F32)
+                taps_in[0, j, rows] = (ends + centre).astype(BF16)
+                taps_in[1, j, rows] = (ends - centre).astype(BF16)
+            return 0
+
+        lax.fori_loop(0, chans // CHUNK, step, 0)
 
     def mix_taps(p):
         def step(t, _):
@@ -338,6 +357,7 @@
         send_halo(img, 0, slice(None))
         sums[...] = jnp.zeros_like(sums)
         load_w_in.wait()
+        mix_taps_in(slice(SIDE, 2 * SIDE))
         load_w_out.wait()
         for p in range(depth):
             mix_taps(p)
@@ -361,8 +381,50 @@
             first = [rows_split(w_in, p, k) for k in range(depth)]
             return [sum((pair[m] for pair in first), []) for m in range(2)]
 
-        own_b, ends_b = both(1)
+        combos = [
+            (1, 2, 1.0, 0, 0), (2, 1, -1.0, 1, 1), (3, 1, -1.0, None, 2),
+            (3, 4, 1.0, 0, 3), (4, 3, -1.0, 1, 0), (2, 4, -1.0, None, 1),
+            (0, 2, -1.0, None, 2), (5, 3, -1.0, None, 3),
+        ]
+        sides = {2: 2, 5: 0, 6: 0, 7: 2}
+
         _, ends_a = both(0)
+        pairs = ((0, 1, 2, 6), (3, 4, 5, 7))
+
+        def wide(stage):
+            ref = (stage + share) % height
+
+            def entry(j, k, q):
+                m = pairs[q][stage]
+                kind = combos[m][3]
+                if kind is None:
+                    tile = tile_of(w_in, sides[m], j, k, 1)
+                else:
+                    tile = lambda: taps_in[kind, j, k * SIDE : (k + 1) * SIDE]
+                return tile, [(ref, lambda: shifted(mixed, m, j, k))]
+
+            return [
+                {q: entry(j, k, q) for q in range(UNITS)} for k in range(depth) for j in range(3)
+            ]
+
+        def mixing_in(stage):
+            return [
+                functools.partial(mix_rounded, pairs[q][stage], *combos[pairs[q][stage]][:3], k)
+                for k in range(parts) for q in range(UNITS)
+            ]
+
+        def split_b(q):
+            lanes = lanes_of(1)
+            a, b = pltpu.matmul_pop(acc[q][share]), pltpu.matmul_pop(acc[q][share + 1])
+            part[share * q, :, lanes] = a + b
+            part[share * q + 1, :, lanes] = a - b
+
+        def finish_b(q, r, ref):
+            lanes = lanes_of(1)
+            value = (part[r, :, lanes] + pltpu.matmul_pop(acc[q][ref])).astype(BF16)
+            mid[1 + r, :, lanes] = value
+            add_stats(value.astype(F32), lanes)
+
         near = (1, height)
         far = [r for r in mine if r not in near]
         for hook in rows_act(img, near, range(slabs), affine):
@@ -372,28 +434,39 @@
         plan.update(spread(rows_act(img, mine, range(slabs, parts), affine), 4, len(start)))
         contract(start, plan)
         later = sum((rows_split(w_in, 0, k)[0] for k in range(1, depth)), [])
-        contract(later)
-        contract(own_b[:LEAD])
+        plan = spread(mixing_in(0), 0, 5)
+        plan.update(spread(mixing_in(1), 5, len(later)))
+        contract(later, plan)
+        steps_b = sum((wide(stage) for stage in range(4)), [])
+        contract(steps_b[:LEAD], spread(mixing_in(2), 0, LEAD))
         wait_halo(img, 0, slice(None))
         contract(
-            own_b[LEAD : LEAD + SOAK],
+            steps_b[LEAD : LEAD + SOAK],
             spread(rows_act(img, halo, range(slabs), affine), 0, SOAK),
         )
         plan = spread(rows_act(img, halo, range(slabs, parts), affine), 0, 2)
         plan.update(spread(kept(0, middle), 3, len(ends_a)))
         contract(ends_a, plan)
         contract(
-            own_b[LEAD + SOAK : LEAD + SOAK + DRAIN],
+            steps_b[LEAD + SOAK : LEAD + SOAK + DRAIN],
             spread(
                 kept(0, outer) + [functools.partial(prepare_stats, gath_a, lanes_of(0))], 0, DRAIN
             ),
         )
         send_stats(gath_a, 1)
         send_halo(mid, 1, lanes_of(0))
-        contract(own_b[LEAD + SOAK + DRAIN :])
-        contract(ends_b, spread(kept(1, middle), 1, len(ends_b)))
-        for hook in kept(1, outer):
-            hook()
+        done = LEAD + SOAK + DRAIN
+        plan = spread(mixing_in(3), 0, 5)
+        plan.update(spread(
+            [functools.partial(split_b, q) for q in range(UNITS)], max(15 - done, 5), 18 - done
+        ))
+        plan.update(spread(
+            [functools.partial(finish_b, 0, 1, 0), functools.partial(finish_b, 1, 2, 0)],
+            20 - done, 23 - done,
+        ))
+        contract(steps_b[done:], plan)
+        finish_b(0, 0, 1)
+        finish_b(1, height - 1, 1)
         prepare_stats(gath_b, lanes_of(1))
         send_stats(gath_b, 2)
         send_halo(mid, 2, lanes_of(1))
@@ -417,13 +490,6 @@
         def save(r, ref):
             for q in range(UNITS):
                 part[r, :, lanes_of(q)] += pltpu.matmul_pop(acc[q][ref])
-
-        combos = [
-            (1, 2, 1.0, 0, 0), (2, 1, -1.0, 1, 1), (3, 1, -1.0, None, 2),
-            (3, 4, 1.0, 0, 3), (4, 3, -1.0, 1, 0), (2, 4, -1.0, None, 1),
-            (0, 2, -1.0, None, 2), (5, 3, -1.0, None, 3),
-        ]
-        sides = {2: 2, 5: 0, 6: 0, 7: 2}
 
         def product(m, p):
             kind, ref = combos[m][3:]
@@ -464,6 +530,19 @@
             late.update(spread(mixing(7) + [functools.partial(put, 2, 1)], 4, 7))
             late.update({8: [functools.partial(put, 0, 2)]})
             opening = plain(1) + plain(2) + mixing(0)
+            if p == depth - 1:
+                top, low = plain(0), plain(5)
+                early = spread(mixing(1) + plain(3), 0, 3)
+                early.update(spread(mixing(2) + plain(4), 3, 6))
+                early.update({6: mixing(3)})
+                early.update(spread(folding(0, 0, 1), 7, 9))
+                late = {
+                    0: mixing(4), 1: top[:1], 2: [functools.partial(put, 1, 2)], 3: top[1:],
+                    4: mixing(5), 5: low[:1], 6: low[1:] + mixing(6),
+                    8: folding(2, 3, 0)[:1], 9: folding(2, 3, 0)[1:] + mixing(7),
+                    11: [functools.partial(put, 2, 1)], 14: [functools.partial(put, 0, 2)],
+                }
+                return opening, steps[:9], early, steps[9:], late, functools.partial(put, height - 1, 3)
             return opening, steps[:15], early, steps[15:], late, functools.partial(put, height - 1, 3)
 
         def ready(p, gath):
@@ -476,12 +555,17 @@
             hook()
         contract(steps, plan)
         wait_halo(mid, 1, lanes_of(0))
-        contract(rest, rest_plan)
+        contract(rest[:TURN], {t: hooks for t, hooks in rest_plan.items() if t < TURN})
         opening, steps, plan, last, last_plan, final = ready(1, gath_b)
-        for hook in opening:
-            hook()
-        plan[2] = plan[2] + [closing]
-        contract(steps, plan)
+        ahead = len(rest) - TURN
+        joined = {t - TURN: list(hooks) for t, hooks in rest_plan.items() if TURN <= t < 8}
+        for t, hooks in spread(opening, 0, ahead).items():
+            joined.setdefault(t, []).extend(hooks)
+        for t, hooks in plan.items():
+            joined.setdefault(t + ahead, []).extend(hooks)
+        joined[ahead + 1] = joined.get(ahead + 1, []) + rest_plan[8]
+        joined[ahead + 3] = joined.get(ahead + 3, []) + [closing]
+        contract(rest[TURN:] + steps, joined)
         wait_halo(mid, 2, lanes_of(1))
         contract(last, last_plan)
         final()
@@ -514,8 +598,9 @@
             pltpu.VMEM((height + 2, width, chans), BF16),
             pltpu.VMEM(conv_in.shape, BF16),
             pltpu.VMEM(conv_out.shape, BF16),
+            pltpu.VMEM((2, 3, chans, SIDE), BF16),
             pltpu.VMEM((chans // SIDE, 2, 3, SIDE, chans), BF16),
-            pltpu.VMEM((8, SIDE // LANES, width + 2 * PAD, LANES), F32),
+            pltpu.VMEM((8, chans // LANES, width + 2 * PAD, LANES), F32),
             pltpu.VMEM((height, width, chans), F32),
             pltpu.VMEM((8, chans), F32),
             pltpu.VMEM((2, 8, chans), F32),
@@ -530,7 +615,7 @@
             pltpu.SemaphoreType.DMA((3,)),
         ],
         compiler_params=pltpu.CompilerParams(
-            collective_id=0, has_side_effects=True, vmem_limit_bytes=44 * 1024 * 1024
+            collective_id=0, has_side_effects=True, vmem_limit_bytes=48 * 1024 * 1024
         ),
     )(*[pin(x) for x in operands])
 

time: 23.1 us -> 22.8 us (0.987)
  Pallas kernels: 22 us -> 21.7 us
    pallas_call x1, Pallas kernels: 22 us -> 21.7 us  [local(): pl.pallas_call(functools.partial(kernel, n), out_shape=jax.ShapeDtypeStru...]
where the time goes in v4:
time: 22.8 us; the launch traced here: 22.6 us
  Pallas kernels  21.7 us (95%)
  local copies, waits for them, and re-layouts  0.97 us (4%)
    pallas_call x1, Pallas kernels, local(): pl.pallas_call(functools.partial(kernel, n), out_shape=jax.ShapeDtypeStru...  21.7 us
    unnamed x1, local copies, waits for them, and re-layouts  0.97 us

profile of v4, /device:TPU:0, one launch (start us, length us, event | category | flops | bytes accessed | tf_op | source)
XLA Modules:
  0.0 22.6 jit_solution(2659255541063150895)
XLA Ops:
  0.0 21.7 %shard_map.82 = bf16[4,256,512]{2,1,0:T(8,128)(2,1)S(1)} custom-call(bf16[4,256,512]{2,1,0:T(8,128)(2,1)} %image.1, f32[1,512]{1,0:T(1,128)} %bitcast.5, f32[1,512]{1,0:T(1,128)} %bitcast.6, bf16[3,3,512,512]{3,2,1,0:T(8,128)(2,1)} %conv_in.1, f32[1,512]{1,0:T(1,128)} %bitcast.7, f32[1,512]{1,0:T(1,128)} %bitcast.8, bf16[3,3,512,512]{3,2,1,0:T(8,128)(2,1)} %conv_out.1, ...), custom_call_target="tpu_custom_call" | custom-call | tf_op jit(solution)/shard_map/pallas_call | solution.py:590
  21.7 1.0 %copy.10 = bf16[4,256,512]{2,1,0:T(8,128)(2,1)} copy(bf16[4,256,512]{2,1,0:T(8,128)(2,1)S(1)} %shard_map.82) | data formatting | bytes 2097152

commit v5 on v4

--- a/solution.py
+++ b/solution.py
@@ -13,10 +13,9 @@
 UNITS = 2
 CHUNK = 32
 PAD = 8
-LEAD = 1
 TURN = 5
 SOAK = 1
-DRAIN = 3
+DRAIN = 2
 MESH = pl.DeviceIdType.MESH
 BF16, F32 = jnp.bfloat16, jnp.float32
 
@@ -354,7 +353,8 @@
         prepare_stats(gath_in, slice(None))
         pl.semaphore_wait(barrier, n - 1)
         send_stats(gath_in, 0)
-        send_halo(img, 0, slice(None))
+        send_halo(img, 0, lanes_of(0))
+        send_halo(img, 3, lanes_of(1))
         sums[...] = jnp.zeros_like(sums)
         load_w_in.wait()
         mix_taps_in(slice(SIDE, 2 * SIDE))
@@ -438,25 +438,26 @@
         plan.update(spread(mixing_in(1), 5, len(later)))
         contract(later, plan)
         steps_b = sum((wide(stage) for stage in range(4)), [])
-        contract(steps_b[:LEAD], spread(mixing_in(2), 0, LEAD))
-        wait_halo(img, 0, slice(None))
+        wait_halo(img, 0, lanes_of(0))
         contract(
-            steps_b[LEAD : LEAD + SOAK],
+            steps_b[:SOAK],
             spread(rows_act(img, halo, range(slabs), affine), 0, SOAK),
         )
+        wait_halo(img, 3, lanes_of(1))
         plan = spread(rows_act(img, halo, range(slabs, parts), affine), 0, 2)
         plan.update(spread(kept(0, middle), 3, len(ends_a)))
         contract(ends_a, plan)
         contract(
-            steps_b[LEAD + SOAK : LEAD + SOAK + DRAIN],
+            steps_b[SOAK : SOAK + DRAIN],
             spread(
                 kept(0, outer) + [functools.partial(prepare_stats, gath_a, lanes_of(0))], 0, DRAIN
             ),
         )
         send_stats(gath_a, 1)
         send_halo(mid, 1, lanes_of(0))
-        done = LEAD + SOAK + DRAIN
-        plan = spread(mixing_in(3), 0, 5)
+        done = SOAK + DRAIN
+        plan = spread(mixing_in(2), 0, 4)
+        plan.update(spread(mixing_in(3), 4, 9))
         plan.update(spread(
             [functools.partial(split_b, q) for q in range(UNITS)], max(15 - done, 5), 18 - done
         ))
@@ -609,8 +610,8 @@
             pltpu.VMEM((n, LANES), F32),
             pltpu.SemaphoreType.DMA((height,)),
             pltpu.SemaphoreType.DMA((3,)),
-            pltpu.SemaphoreType.DMA((3, 2)),
-            pltpu.SemaphoreType.DMA((3, 2)),
+            pltpu.SemaphoreType.DMA((4, 2)),
+            pltpu.SemaphoreType.DMA((4, 2)),
             pltpu.SemaphoreType.DMA((3,)),
             pltpu.SemaphoreType.DMA((3,)),
         ],

time: 22.8 us -> 22.8 us (level)
  no operation moved by 1% of the time
where the time goes in v5:
time: 22.8 us; the launch traced here: 22.7 us
  Pallas kernels  21.7 us (95%)
  local copies, waits for them, and re-layouts  0.97 us (4%)
    pallas_call x1, Pallas kernels, local(): pl.pallas_call(functools.partial(kernel, n), out_shape=jax.ShapeDtypeStru...  21.7 us
    unnamed x1, local copies, waits for them, and re-layouts  0.97 us

profile of v5, /device:TPU:0, one launch (start us, length us, event | category | flops | bytes accessed | tf_op | source)
XLA Modules:
  0.0 22.7 jit_solution(15989870053578188062)
XLA Ops:
  0.0 21.7 %shard_map.82 = bf16[4,256,512]{2,1,0:T(8,128)(2,1)S(1)} custom-call(bf16[4,256,512]{2,1,0:T(8,128)(2,1)} %image.1, f32[1,512]{1,0:T(1,128)} %bitcast.5, f32[1,512]{1,0:T(1,128)} %bitcast.6, bf16[3,3,512,512]{3,2,1,0:T(8,128)(2,1)} %conv_in.1, f32[1,512]{1,0:T(1,128)} %bitcast.7, f32[1,512]{1,0:T(1,128)} %bitcast.8, bf16[3,3,512,512]{3,2,1,0:T(8,128)(2,1)} %conv_out.1, ...), custom_call_target="tpu_custom_call" | custom-call | tf_op jit(solution)/shard_map/pallas_call | solution.py:591
  21.7 1.0 %copy.10 = bf16[4,256,512]{2,1,0:T(8,128)(2,1)} copy(bf16[4,256,512]{2,1,0:T(8,128)(2,1)S(1)} %shard_map.82) | data formatting | bytes 2097152

commit v6 on v4

--- a/solution.py
+++ b/solution.py
@@ -51,7 +51,7 @@
 
 def kernel(n, image, gain_in, shift_in, conv_in, gain_mid, shift_mid, conv_out, bias_out, out,
            img, act, mid, w_in, w_out, taps_in, taps, mixed, part, vec, sums, gath_in, gath_a, gath_b,
-           img_sem, load_sem, halo_send, halo_recv, stat_send, stat_recv):
+           halo_send, halo_recv, stat_send, stat_recv):
     me = lax.axis_index("rows")
     height, width, chans = image.shape
     size = chans // GROUPS
@@ -60,15 +60,6 @@
     depth = chans // SIDE
     slabs = SIDE // LANES
     share = height // UNITS
-
-    order = [0, height - 1] + list(range(1, height - 1))
-    loads = {
-        r: pltpu.make_async_copy(image.at[r], img.at[1 + r], img_sem.at[r]) for r in order
-    }
-    for r in order:
-        loads[r].start()
-    load_w_in = pltpu.make_async_copy(conv_in, w_in, load_sem.at[0])
-    load_w_out = pltpu.make_async_copy(conv_out, w_out, load_sem.at[1])
 
     barrier = pltpu.get_barrier_semaphore()
     for d in range(1, n):
@@ -230,7 +221,16 @@
 
         lax.fori_loop(0, SIDE // CHUNK, step, 0)
 
-    def body(*accs):
+    def body(img_sem, load_sem, *accs):
+        order = [0, height - 1] + list(range(1, height - 1))
+        loads = {
+            r: pltpu.make_async_copy(image.at[r], img.at[1 + r], img_sem.at[r]) for r in order
+        }
+        for r in order:
+            loads[r].start()
+        load_w_in = pltpu.make_async_copy(conv_in, w_in, load_sem.at[0])
+        load_w_out = pltpu.make_async_copy(conv_out, w_out, load_sem.at[1])
+
         acc = [accs[q * height : (q + 1) * height] for q in range(UNITS)]
 
         zero = jnp.zeros((SIDE, SIDE), BF16)
@@ -574,7 +574,10 @@
         all_sent(gath_b, 2)
 
     pl.run_scoped(
-        body, *[pltpu.ACC(q)((width, SIDE), F32) for q in range(UNITS) for _ in range(height)]
+        body,
+        pltpu.SemaphoreType.DMA((height,)),
+        pltpu.SemaphoreType.DMA((3,)),
+        *[pltpu.ACC(q)((width, SIDE), F32) for q in range(UNITS) for _ in range(height)],
     )
 
 
@@ -607,8 +610,6 @@
             pltpu.VMEM((n, LANES), F32),
             pltpu.VMEM((n, LANES), F32),
             pltpu.VMEM((n, LANES), F32),
-            pltpu.SemaphoreType.DMA((height,)),
-            pltpu.SemaphoreType.DMA((3,)),
             pltpu.SemaphoreType.DMA((3, 2)),
             pltpu.SemaphoreType.DMA((3, 2)),
             pltpu.SemaphoreType.DMA((3,)),

time: 22.8 us -> 22.7 us (level)
  no operation moved by 1% of the time
where the time goes in v6:
time: 22.7 us; the launch traced here: 22.5 us
  Pallas kernels  21.5 us (95%)
  local copies, waits for them, and re-layouts  0.97 us (4%)
    pallas_call x1, Pallas kernels, local(): pl.pallas_call(functools.partial(kernel, n), out_shape=jax.ShapeDtypeStru...  21.5 us
    unnamed x1, local copies, waits for them, and re-layouts  0.97 us

profile of v6, /device:TPU:0, one launch (start us, length us, event | category | flops | bytes accessed | tf_op | source)
XLA Modules:
  0.0 22.5 jit_solution(9998325245638775219)
XLA Ops:
  0.0 21.5 %shard_map.82 = bf16[4,256,512]{2,1,0:T(8,128)(2,1)S(1)} custom-call(bf16[4,256,512]{2,1,0:T(8,128)(2,1)} %image.1, f32[1,512]{1,0:T(1,128)} %bitcast.5, f32[1,512]{1,0:T(1,128)} %bitcast.6, bf16[3,3,512,512]{3,2,1,0:T(8,128)(2,1)} %conv_in.1, f32[1,512]{1,0:T(1,128)} %bitcast.7, f32[1,512]{1,0:T(1,128)} %bitcast.8, bf16[3,3,512,512]{3,2,1,0:T(8,128)(2,1)} %conv_out.1, ...), custom_call_target="tpu_custom_call" | custom-call | tf_op jit(solution)/shard_map/pallas_call | solution.py:593
  21.6 1.0 %copy.10 = bf16[4,256,512]{2,1,0:T(8,128)(2,1)} copy(bf16[4,256,512]{2,1,0:T(8,128)(2,1)S(1)} %shard_map.82) | data formatting | bytes 2097152
